TPU v7x, 128 devices: a whole 4x4x4 slice. The times are simulated.
128 devices in a mesh: gz: 4 (over x), gy: 4 (over z), gx: 8 (over y, core).
Axes of the slice: x: 4, y: 4, z: 4, core: 2. Of those that a mesh axis runs over, the one named last changes fastest.
Arguments:
- spins: float32 [2, 64, 192, 1024], P(None, 'gz', 'gy', 'gx'), may hold values from -6 to 6
- kicks: float32 [2, 2, 64, 192, 1024], P(None, None, 'gz', 'gy', 'gx'), may hold values from -6 to 6
- stiffness: float32 [64, 192, 1024], P('gz', 'gy', 'gx'), may hold values from 0.1 to 11, as said below
Outputs:
- final_spins: float32 [2, 64, 192, 1024], P(None, 'gz', 'gy', 'gx')
- section_energy: float32 [16], replicated
Inputs may be any that keep to these rules, and one draw needn't show every extreme that they name: `stiffness`: positive coupling strengths.
All inputs are finite; a program needn't handle non-finite values.
Results may differ from a plain program's by a relative error of at most 0.0001.
Values sent between devices are 32-bit elements; how exact they have to be, the bound alone decides.
A program may use at most 128 MiB of HBM per device.

v0:
```python
import functools

import jax
import jax.numpy as jnp
from jax import lax
from jax.experimental import pallas as pl
from jax.experimental.pallas import tpu as pltpu
from jax.sharding import PartitionSpec as P

MESH = pl.DeviceIdType.MESH
F32 = jnp.float32
NZ, NY, NX = 16, 48, 128
PITCH = 56
ROWS = 19 * PITCH
TILES = 7

MESSAGES = {
    "Z": ((-1, 0, 0), 256, 112),
    "z": ((1, 0, 0), 96, 96),
    "Y": ((0, -1, 0), 96, 48),
    "y": ((0, 1, 0), 32, 32),
    "ZY": ((-1, -1, 0), 24, 24),
    "Zy": ((-1, 1, 0), 8, 8),
    "zY": ((1, -1, 0), 8, 8),
    "X": ((0, 0, -1), 40, 16),
    "XZ": ((-1, 0, -1), 40, 16),
    "XY": ((0, -1, -1), 40, 16),
    "XZY": ((-1, -1, -1), 40, 16),
    "Xz": ((1, 0, -1), 16, 16),
    "Xy": ((0, 1, -1), 16, 16),
    "XZy": ((-1, 1, -1), 16, 16),
    "XzY": ((1, -1, -1), 16, 16),
    "x": ((0, 0, 1), 16, 16),
    "xZ": ((-1, 0, 1), 16, 16),
    "xY": ((0, -1, 1), 16, 16),
    "xZY": ((-1, -1, 1), 16, 16),
}
NAMES = list(MESSAGES)
COUNT = len(NAMES)


def offsets(round_index):
    start, table = 0, {}
    for name in NAMES:
        size = MESSAGES[name][1 + round_index]
        table[name] = (start, size)
        start += size
    return table, start


TABLE_A, SIZE_A = offsets(0)
TABLE_B, SIZE_B = offsets(1)


def row(z, y):
    return (z + 1) * PITCH + y


def roll(v, shift, axis=1):
    shift = shift % v.shape[axis]
    return v if shift == 0 else pltpu.roll(v, shift, axis)


def kernel(dims, spins, kicks, stiff, out, energy_out, S, J, K, XH, send_a, recv_a, send_b, recv_b, EN, ebuf, erow,
           load_sem, out_sem, sa_sem, ra_sem, sb_sem, rb_sem, es_sem, er_sem):
    nz, ny, nx = dims
    total = nz * ny * nx
    me = (lax.axis_index("gz"), lax.axis_index("gy"), lax.axis_index("gx"))

    def device(step):
        return tuple(lax.rem(m + (d % n), n) for m, d, n in zip(me, step, dims))

    lane = lax.broadcasted_iota(jnp.int32, (8, 128), 1)
    sub = lax.broadcasted_iota(jnp.int32, (8, 128), 0)
    zi = (lane * 9363) >> 16
    tile = lane - zi * 7

    def load(z, which):
        dst = pl.ds(pl.multiple_of((z + 1) * PITCH, 8), NY)
        if which == 0:
            return pltpu.make_async_copy(spins.at[:, z], S.at[:, dst, :], load_sem.at[0, z])
        if which == 1:
            return pltpu.make_async_copy(stiff.at[z], J.at[dst, :], load_sem.at[1, z])
        w = which - 2
        return pltpu.make_async_copy(kicks.at[w, :, z], K.at[pl.ds(2 * w, 2), dst, :], load_sem.at[which, z])

    def each(f):
        def step(z, carry):
            f(z)
            return carry

        lax.fori_loop(0, NZ, step, 0)

    for which in range(4):
        each(lambda z, which=which: load(z, which).start())

    barrier = pltpu.get_barrier_semaphore()
    steps = [MESSAGES[name][0] for name in NAMES]
    steps += [(0, 0, d) for d in range(2, nx - 1)]
    for s in steps:
        pl.semaphore_signal(barrier, inc=1, device_id=device(tuple(-d for d in s)), device_id_type=MESH)

    for which in range(3):
        each(lambda z, which=which: load(z, which).wait())

    zero_plane = jnp.zeros((PITCH, 128), F32)
    for c in range(2):
        S[c, pl.ds(18 * PITCH, PITCH), :] = zero_plane
        S[c, pl.ds(row(0, 49), NZ, stride=PITCH), :] = jnp.zeros((NZ, 128), F32)
        S[c, pl.ds(row(16, 49), 1), :] = jnp.zeros((1, 128), F32)

    lane3 = lane - ((lane * 21846) >> 16) * 3
    group = [((lane - r + 1) * 21846) >> 16 for r in range(3)]
    own_tiles = [(z + 1) * TILES + t for z in range(NZ) for t in range(6)]

    def pack_spins():
        cols = []
        for c in range(2):
            acc = [jnp.zeros((8, 128), F32) for _ in range(3)]
            for q in own_tiles:
                r = q % 3
                v = roll(S[c, pl.ds(8 * q, 8), :], q)
                acc[r] = jnp.where(group[r] == q // 3, v, acc[r])

            def pick(shift):
                a = [roll(v, shift) for v in acc]
                return jnp.where(lane3 == 0, a[0], jnp.where(lane3 == 1, a[1], a[2]))

            cols.append((pick(0), pick(-1), pick(1)))
        return [[cols[c][k] for c in range(2)] for k in range(3)]

    def pack_first(read):
        acc = jnp.zeros((8, 128), F32)
        for q in own_tiles:
            acc = jnp.where(lane == q, roll(read(8 * q), q), acc)
        return acc

    def zplus(v):
        return roll(v, -7)

    def yplus(v):
        return roll(v, -1, 0)

    def copies(send, recv, table, ssem, rsem):
        result = {}
        for i, name in enumerate(NAMES):
            start, size = table[name]
            part = pl.ds(start, size)
            result[name] = pltpu.make_async_remote_copy(
                src_ref=send.at[part, :],
                dst_ref=recv.at[part, :],
                send_sem=ssem.at[i],
                recv_sem=rsem.at[i],
                device_id=device(MESSAGES[name][0]),
                device_id_type=MESH,
            )
        return result

    def put(send, table, name, at, value):
        send[pl.ds(table[name][0] + at, value.shape[0]), :] = value

    def get(recv, table, name, at, size=8):
        return recv[pl.ds(table[name][0] + at, size), :]

    copies_a = copies(send_a, recv_a, TABLE_A, sa_sem, ra_sem)
    copies_b = copies(send_b, recv_b, TABLE_B, sb_sem, rb_sem)

    def build(send, table, w):
        first = w == 0
        n = 5 if first else 2
        J0 = J[pl.ds(row(0, 0), NY), :]
        for c in range(2):
            kc = K[2 * w + c, pl.ds(row(0, 0), NY), :] + J0 * S[c, pl.ds(row(1, 0), NY), :]
            put(send, table, "Z", (n - 2 + c) * NY, kc)
            if first:
                put(send, table, "Z", c * NY, S[c, pl.ds(row(0, 0), NY), :])
            put(send, table, "z", c * NY, S[c, pl.ds(row(15, 0), NY), :])
        if first:
            put(send, table, "Z", 2 * NY, J0)
        rows0 = pl.ds(row(0, 0), NZ, stride=PITCH)
        rows1 = pl.ds(row(0, 1), NZ, stride=PITCH)
        rows47 = pl.ds(row(0, 47), NZ, stride=PITCH)
        Jy = J[rows0, :]
        for c in range(2):
            kc = K[2 * w + c, rows0, :] + Jy * S[c, rows1, :]
            put(send, table, "Y", (n - 2 + c) * NZ, kc)
            if first:
                put(send, table, "Y", c * NZ, S[c, rows0, :])
            put(send, table, "y", c * NZ, S[c, rows47, :])
        if first:
            put(send, table, "Y", 2 * NZ, Jy)
        at = pl.ds(row(0, 0), 1)
        for c in range(2):
            kc = K[2 * w + c, at, :] + J[at, :] * (S[c, pl.ds(row(1, 0), 1), :] + S[c, pl.ds(row(0, 1), 1), :])
            put(send, table, "ZY", n - 2 + c, kc)
            if first:
                put(send, table, "ZY", c, S[c, at, :])
            put(send, table, "Zy", c, S[c, pl.ds(row(0, 47), 1), :])
            put(send, table, "zY", c, S[c, pl.ds(row(15, 0), 1), :])
        if first:
            put(send, table, "ZY", 2, J[at, :])

    def build_columns(send, table, w, PJ, PK):
        first = w == 0
        n = 5 if first else 2
        PS, PT, PR = pack_spins()
        for c in range(2):
            zs, ys = zplus(PS[c]), yplus(PS[c])
            sums = {"X": PT[c], "XZ": PT[c] + zs, "XY": PT[c] + ys, "XZY": PT[c] + zs + ys}
            for name, value in sums.items():
                put(send, table, name, (n - 2 + c) * 8, PK[c] + PJ * value)
                if first:
                    put(send, table, name, c * 8, PS[c])
            for name in ("Xz", "Xy", "XZy", "XzY"):
                put(send, table, name, c * 8, PS[c])
            for name in ("x", "xZ", "xY", "xZY"):
                put(send, table, name, c * 8, PR[c])
            put(send, table, "Z", n * NY + c * 8, PR[c])
            put(send, table, "Y", n * NZ + c * 8, PR[c])
            put(send, table, "ZY", 8 + c * 8, PR[c])
        if first:
            for name in ("X", "XZ", "XY", "XZY"):
                put(send, table, name, 16, PJ)
        return PR

    def merge_faces(recv, table, w):
        first = w == 0
        n = 5 if first else 2
        plane = pl.ds(row(16, 0), NY)
        rows48 = pl.ds(row(0, 48), NZ, stride=PITCH)
        at = pl.ds(row(16, 48), 1)
        for c in range(2):
            K[2 * w + c, plane, :] = get(recv, table, "Z", (n - 2 + c) * NY, NY)
            K[2 * w + c, rows48, :] = get(recv, table, "Y", (n - 2 + c) * NZ, NZ)
            K[2 * w + c, at, :] = get(recv, table, "ZY", n - 2 + c, 1)
            if first:
                S[c, plane, :] = get(recv, table, "Z", c * NY, NY)
                S[c, rows48, :] = get(recv, table, "Y", c * NZ, NZ)
                S[c, at, :] = get(recv, table, "ZY", c, 1)
            S[c, pl.ds(row(-1, 0), NY), :] = get(recv, table, "z", c * NY, NY)
            S[c, pl.ds(row(0, -1), NZ, stride=PITCH), :] = get(recv, table, "y", c * NZ, NZ)
            S[c, pl.ds(row(16, -1), 1), :] = get(recv, table, "Zy", c, 1)
            S[c, pl.ds(row(-1, 48), 1), :] = get(recv, table, "zY", c, 1)
        if first:
            J[plane, :] = get(recv, table, "Z", 2 * NY, NY)
            J[rows48, :] = get(recv, table, "Y", 2 * NZ, NZ)
            J[at, :] = get(recv, table, "ZY", 2, 1)

    at_z = (zi == 17) & (tile < 6)
    at_y = (tile == 6) & (sub == 0) & (zi >= 1) & (zi <= 16)
    at_zy = (zi == 17) & (tile == 6) & (sub == 0)
    at_zm = (zi == 0) & (tile < 6)
    at_ym = (tile == 6) & (sub == 7) & (zi <= 15)
    at_zym = (lane == 118) & (sub == 7)
    at_yzm = (lane == 6) & (sub == 0)

    def upper(base, vz, vy, vzy):
        base = jnp.where(at_z, roll(vz, 112), base)
        base = jnp.where(at_y, roll(vy, 6), base)
        return jnp.where(at_zy, roll(vzy, 118), base)

    def lower(base, recv, table, c):
        base = jnp.where(at_zm, roll(get(recv, table, "Xz", c * 8), -112), base)
        base = jnp.where(at_ym, roll(get(recv, table, "Xy", c * 8), -6), base)
        base = jnp.where(at_zym, roll(get(recv, table, "XZy", c * 8), 106), base)
        return jnp.where(at_yzm, roll(get(recv, table, "XzY", c * 8), -106), base)

    def merge_columns(recv, table, w, PR, ES, EJ):
        first = w == 0
        n = 5 if first else 2

        def ext(at):
            v = [get(recv, table, name, at) for name in ("X", "XZ", "XY", "XZY")]
            return upper(*v)

        EK = [ext((n - 2 + c) * 8) for c in range(2)]
        if first:
            ES = [ext(c * 8) for c in range(2)]
            EJ = ext(16)
        ES = [lower(ES[c], recv, table, c) for c in range(2)]
        HM = [upper(*[get(recv, table, name, c * 8) for name in ("x", "xZ", "xY", "xZY")]) for c in range(2)]
        PM = [
            upper(
                PR[c],
                get(recv, table, "Z", n * NY + c * 8),
                get(recv, table, "Y", n * NZ + c * 8),
                get(recv, table, "ZY", 8 + c * 8),
            )
            for c in range(2)
        ]
        return EK, ES, EJ, HM, PM

    def shift_up(v):
        v = roll(v, 1, 0)
        return jnp.where(sub == 0, roll(v, 1), v)

    def shift_down(v):
        v = roll(v, -1, 0)
        return jnp.where(sub == 7, roll(v, -1), v)

    inside = (zi >= 1) & (zi <= 17) & ((tile < 6) | (sub == 0))

    def update_column(EK, ES, EJ, PM):
        for zp in range(2):
            for yp in range(2):
                member = inside & ((zi & 1) == 1 - zp) & ((sub & 1) == yp)
                local = []
                for c in range(2):
                    v = ES[c]
                    above = jnp.where(lane < 17 * TILES, roll(v, -7), 0.0)
                    near = shift_up(v) + shift_down(v) + roll(v, 7) + above + PM[c]
                    local.append(EJ * near + EK[c])
                scale = lax.rsqrt(1.0 + (local[0] * local[0] + local[1] * local[1]))
                ES = [jnp.where(member, local[c] * scale, ES[c]) for c in range(2)]
        return ES

    def spread_columns(HM, ES):
        for c in range(2):
            e = roll(ES[c], -1)
            even = (lane & 1) == 0
            mixed = [jnp.where(even, HM[c], e), jnp.where(even, e, HM[c])]
            for q in range(TILES, 18 * TILES):
                XH[c, pl.ds(8 * q, 8), :] = roll(mixed[q % 2], -q)

    def update(w, base, n, stride, xp):
        def at(off):
            return pl.ds(base + off, n, stride=stride) if n > 1 else pl.ds(base + off, 1)

        lanes = lax.broadcasted_iota(jnp.int32, (n, 128), 1)
        member = (lanes & 1) == xp
        stiffness = J[at(0), :]
        local, centre = [], []
        for c in range(2):
            v = S[c, at(0), :]
            edge = XH[c, at(0), :]
            left, right = roll(v, 1), roll(v, -1)
            if xp == 0:
                left = jnp.where(lanes == 0, edge, left)
            else:
                right = jnp.where(lanes == 127, edge, right)
            near = (S[c, at(-1), :] + S[c, at(1), :]) + (S[c, at(-PITCH), :] + S[c, at(PITCH), :]) + (left + right)
            local.append(stiffness * near + K[2 * w + c, at(0), :])
            centre.append(v)
        q = local[0] * local[0] + local[1] * local[1]
        scale = lax.rsqrt(1.0 + q)
        for c in range(2):
            S[c, at(0), :] = jnp.where(member, local[c] * scale, centre[c])
        return q * scale

    def section(w, zp, yp, xp):
        energy = None
        for z in range(zp, NZ + 1 - zp, 2):
            e = update(w, row(z, yp), 24, 2, xp)
            if z < NZ:
                energy = e if energy is None else energy + e
        if yp == 0:
            update(w, row(zp, 48), 8, 2 * PITCH, xp)
            if zp == 0:
                update(w, row(16, 48), 1, 1, xp)
        energy = energy[0:8] + energy[8:16] + energy[16:24]
        t = 8 * w + 4 * zp + 2 * yp + xp
        EN[t] = jnp.where((lane & 1) == xp, energy, 0.0)

    build(send_a, TABLE_A, 0)
    PJ = pack_first(lambda r: J[pl.ds(r, 8), :])
    PK = [pack_first(lambda r, c=c: K[c, pl.ds(r, 8), :]) for c in range(2)]
    PR = build_columns(send_a, TABLE_A, 0, PJ, PK)
    pl.semaphore_wait(barrier, len(steps))
    for name in NAMES:
        copies_a[name].start()
    each(lambda z: load(z, 3).wait())
    PK = [pack_first(lambda r, c=c: K[2 + c, pl.ds(r, 8), :]) for c in range(2)]
    for name in NAMES:
        copies_a[name].wait_recv()
    merge_faces(recv_a, TABLE_A, 0)
    EK, ES, EJ, HM, PM = merge_columns(recv_a, TABLE_A, 0, PR, None, None)
    ES = update_column(EK, ES, EJ, PM)
    spread_columns(HM, ES)
    for t in range(8):
        section(0, t // 4, t // 2 % 2, t % 2)

    build(send_b, TABLE_B, 1)
    PR = build_columns(send_b, TABLE_B, 1, PJ, PK)
    for name in NAMES:
        copies_b[name].start()
    for name in NAMES:
        copies_a[name].wait_send()
    for name in NAMES:
        copies_b[name].wait_recv()
    merge_faces(recv_b, TABLE_B, 1)
    EK, ES, EJ, HM, PM = merge_columns(recv_b, TABLE_B, 1, PR, ES, EJ)
    ES = update_column(EK, ES, EJ, PM)
    spread_columns(HM, ES)
    for t in range(8):
        section(1, t // 4, t // 2 % 2, t % 2)

    def store(z):
        src = pl.ds(pl.multiple_of((z + 1) * PITCH, 8), NY)
        return pltpu.make_async_copy(S.at[:, src, :], out.at[:, z], out_sem.at[z])

    sums = jnp.sum(jnp.sum(EN[...], axis=1), axis=1, keepdims=True)
    diagonal = lax.broadcasted_iota(jnp.int32, (16, 128), 0) == lax.broadcasted_iota(jnp.int32, (16, 128), 1)
    mine = jnp.sum(jnp.where(diagonal, jnp.broadcast_to(sums, (16, 128)), 0.0), axis=0, keepdims=True)
    index = (me[0] * ny + me[1]) * nx + me[2]
    erow[0] = mine
    ebuf[index] = mine

    def share(i, carry):
        to = lax.rem(index + i, total)
        pltpu.make_async_remote_copy(
            src_ref=erow.at[0],
            dst_ref=ebuf.at[index],
            send_sem=es_sem,
            recv_sem=er_sem,
            device_id=(to // (ny * nx), lax.rem(to // nx, ny), lax.rem(to, nx)),
            device_id_type=MESH,
        ).start()
        return carry

    lax.fori_loop(1, total, share, 0)
    each(lambda z: store(z).start())
    for name in NAMES:
        copies_b[name].wait_send()
    rest = pl.ds(0, total - 1)
    done = pltpu.make_async_remote_copy(
        src_ref=ebuf.at[rest],
        dst_ref=ebuf.at[rest],
        send_sem=es_sem,
        recv_sem=er_sem,
        device_id=me,
        device_id_type=MESH,
    )
    done.wait_recv()
    whole = ebuf[0]
    for i in range(1, total):
        whole = whole + ebuf[i]
    sites = float(8 // 8 * (NZ * nz) * (NY * ny) * (NX * nx) // 8)
    energy_out[...] = -whole / sites
    done.wait_send()
    each(lambda z: store(z).wait())


def body(dims, spins, kicks, stiffness):
    hbm = pl.BlockSpec(memory_space=pl.ANY)
    total = dims[0] * dims[1] * dims[2]
    vmem, dma = pltpu.VMEM, pltpu.SemaphoreType.DMA
    final, energy = pl.pallas_call(
        functools.partial(kernel, dims),
        out_shape=(
            jax.ShapeDtypeStruct((2, NZ, NY, NX), F32),
            jax.ShapeDtypeStruct((1, 128), F32),
        ),
        in_specs=[hbm] * 3,
        out_specs=(hbm, pl.BlockSpec(memory_space=vmem)),
        scratch_shapes=[
            vmem((2, ROWS, 128), F32),
            vmem((ROWS, 128), F32),
            vmem((4, ROWS, 128), F32),
            vmem((2, ROWS, 128), F32),
            vmem((SIZE_A, 128), F32),
            vmem((SIZE_A, 128), F32),
            vmem((SIZE_B, 128), F32),
            vmem((SIZE_B, 128), F32),
            vmem((16, 8, 128), F32),
            vmem((total, 1, 128), F32),
            vmem((1, 1, 128), F32),
            dma((4, NZ)),
            dma((NZ,)),
            dma((COUNT,)),
            dma((COUNT,)),
            dma((COUNT,)),
            dma((COUNT,)),
            dma,
            dma,
        ],
        compiler_params=pltpu.CompilerParams(collective_id=0, has_side_effects=True),
    )(spins, kicks, stiffness)
    return final, energy[0, :16]


def solution(mesh):
    dims = tuple(mesh.shape[a] for a in ("gz", "gy", "gx"))
    return jax.shard_map(
        functools.partial(body, dims),
        mesh=mesh,
        in_specs=(P(None, "gz", "gy", "gx"), P(None, None, "gz", "gy", "gx"), P("gz", "gy", "gx")),
        out_specs=(P(None, "gz", "gy", "gx"), P()),
        check_vma=False,
    )
```

profile of v0, /device:TPU:1, one launch (start us, length us, event | category | flops | bytes accessed | tf_op | source)
XLA Modules:
  0.0 39.3 jit_solution(5619414709836610818)
XLA Ops:
  0.6 35.5 %shard_map.50 = (f32[2,16,48,128]{3,2,1,0:T(8,128)}, f32[1,128]{1,0:T(1,128)}) custom-call(f32[2,16,48,128]{3,2,1,0:T(8,128)} %spins.1, f32[2,2,16,48,128]{4,3,2,1,0:T(8,128)} %kicks.1, f32[16,48,128]{2,1,0:T(8,128)} %stiff.1), custom_call_target="tpu_custom_call" | custom-call | tf_op jit(solution)/shard_map/pallas_call | solution.py:447
  36.2 1.1 %slice_bitcast_fusion = f32[16]{0:T(128)} fusion(f32[1,128]{1,0:T(1,128)} %get-tuple-element.5), kind=kLoop, calls=%fused_computation | loop fusion | bytes 128 | tf_op jit(solution)/shard_map/squeeze | solution.py:478
  37.3 2.1 %copy.6 = f32[2,16,48,128]{3,2,1,0:T(8,128)} copy(f32[2,16,48,128]{3,2,1,0:T(8,128)} %get-tuple-element.8) | data formatting | bytes 1572864
where the time goes:
time: 39.6 us; the launch traced here: 39.3 us
  Pallas kernels  35.5 us (90%)
  local copies, waits for them, and re-layouts  3.15 us (8%)
  between operations  0.64 us (2%)
    pallas_call x1, Pallas kernels, body(): pl.pallas_call(functools.partial(kernel, dims), out_shape=(jax.ShapeDtype...  35.5 us
    unnamed x1, local copies, waits for them, and re-layouts  2.06 us
    squeeze x1, local copies, waits for them, and re-layouts, body(): return (final, energy[0, :16])  1.09 us

commit v1 on v0

--- a/solution.py
+++ b/solution.py
@@ -15,28 +15,32 @@
 TILES = 7
 
 MESSAGES = {
-    "Z": ((-1, 0, 0), 256, 112),
-    "z": ((1, 0, 0), 96, 96),
-    "Y": ((0, -1, 0), 96, 48),
-    "y": ((0, 1, 0), 32, 32),
-    "ZY": ((-1, -1, 0), 24, 24),
+    "XZY": ((-1, -1, -1), 8, 8),
+    "XZy": ((-1, 1, -1), 8, 8),
+    "XzY": ((1, -1, -1), 8, 8),
+    "xZY": ((-1, -1, 1), 8, 8),
+    "ZY": ((-1, -1, 0), 8, 8),
     "Zy": ((-1, 1, 0), 8, 8),
     "zY": ((1, -1, 0), 8, 8),
+    "XZ": ((-1, 0, -1), 8, 8),
+    "XY": ((0, -1, -1), 8, 8),
+    "Xz": ((1, 0, -1), 8, 8),
+    "Xy": ((0, 1, -1), 8, 8),
+    "xZ": ((-1, 0, 1), 8, 8),
+    "xY": ((0, -1, 1), 8, 8),
+    "PZ": ((-1, 0, 0), 8, 8),
+    "PY": ((0, -1, 0), 8, 8),
     "X": ((0, 0, -1), 40, 16),
-    "XZ": ((-1, 0, -1), 40, 16),
-    "XY": ((0, -1, -1), 40, 16),
-    "XZY": ((-1, -1, -1), 40, 16),
-    "Xz": ((1, 0, -1), 16, 16),
-    "Xy": ((0, 1, -1), 16, 16),
-    "XZy": ((-1, 1, -1), 16, 16),
-    "XzY": ((1, -1, -1), 16, 16),
     "x": ((0, 0, 1), 16, 16),
-    "xZ": ((-1, 0, 1), 16, 16),
-    "xY": ((0, -1, 1), 16, 16),
-    "xZY": ((-1, -1, 1), 16, 16),
+    "Z": ((-1, 0, 0), 240, 96),
+    "z": ((1, 0, 0), 96, 96),
+    "Y": ((0, -1, 0), 80, 32),
+    "y": ((0, 1, 0), 32, 32),
 }
 NAMES = list(MESSAGES)
 COUNT = len(NAMES)
+FACES = ("Zy", "zY", "Z", "z", "Y", "y")
+COLUMNS = [name for name in NAMES if name not in FACES]
 
 
 def offsets(round_index):
@@ -62,7 +66,7 @@
 
 
 def kernel(dims, spins, kicks, stiff, out, energy_out, S, J, K, XH, send_a, recv_a, send_b, recv_b, EN, ebuf, erow,
-           load_sem, out_sem, sa_sem, ra_sem, sb_sem, rb_sem, es_sem, er_sem):
+           load_sem, sa_sem, ra_sem, sb_sem, rb_sem, es_sem, er_sem):
     nz, ny, nx = dims
     total = nz * ny * nx
     me = (lax.axis_index("gz"), lax.axis_index("gy"), lax.axis_index("gx"))
@@ -95,7 +99,7 @@
         each(lambda z, which=which: load(z, which).start())
 
     barrier = pltpu.get_barrier_semaphore()
-    steps = [MESSAGES[name][0] for name in NAMES]
+    steps = sorted({MESSAGES[name][0] for name in NAMES})
     steps += [(0, 0, d) for d in range(2, nx - 1)]
     for s in steps:
         pl.semaphore_signal(barrier, inc=1, device_id=device(tuple(-d for d in s)), device_id_type=MESH)
@@ -200,27 +204,47 @@
         if first:
             put(send, table, "ZY", 2, J[at, :])
 
+    def by_lanes(values, shift=0):
+        acc = values[0]
+        for k in range(1, len(values)):
+            acc = jnp.where((lane >> 4) == k, roll(values[k], 16 * k), acc)
+        return acc
+
+    def by_rows(values):
+        acc = values[0]
+        for k in range(1, len(values)):
+            acc = jnp.where(sub == k, roll(values[k], k, 0), acc)
+        return acc
+
     def build_columns(send, table, w, PJ, PK):
         first = w == 0
-        n = 5 if first else 2
         PS, PT, PR = pack_spins()
+        parts = {name: [] for name in ("X", "XZ", "XY", "XZY")}
         for c in range(2):
             zs, ys = zplus(PS[c]), yplus(PS[c])
             sums = {"X": PT[c], "XZ": PT[c] + zs, "XY": PT[c] + ys, "XZY": PT[c] + zs + ys}
             for name, value in sums.items():
-                put(send, table, name, (n - 2 + c) * 8, PK[c] + PJ * value)
-                if first:
-                    put(send, table, name, c * 8, PS[c])
-            for name in ("Xz", "Xy", "XZy", "XzY"):
-                put(send, table, name, c * 8, PS[c])
-            for name in ("x", "xZ", "xY", "xZY"):
-                put(send, table, name, c * 8, PR[c])
-            put(send, table, "Z", n * NY + c * 8, PR[c])
-            put(send, table, "Y", n * NZ + c * 8, PR[c])
-            put(send, table, "ZY", 8 + c * 8, PR[c])
+                parts[name].append(PK[c] + PJ * value)
         if first:
-            for name in ("X", "XZ", "XY", "XZY"):
-                put(send, table, name, 16, PJ)
+            parts = {name: PS + [PJ] + value for name, value in parts.items()}
+        put(send, table, "XZY", 0, by_rows(parts["XZY"]))
+        put(send, table, "XZ", 0, by_lanes(parts["XZ"]))
+        put(send, table, "XY", 0, by_rows(parts["XY"]))
+        for k, value in enumerate(parts["X"]):
+            put(send, table, "X", 8 * k, value)
+        last = jnp.where(sub == 6, roll(PS[1], -1, 0), PS[0])
+        put(send, table, "XZy", 0, last)
+        put(send, table, "Xy", 0, last)
+        put(send, table, "XzY", 0, by_rows(PS))
+        put(send, table, "Xz", 0, jnp.where((lane >> 4) == 6, roll(PS[1], -16), PS[0]))
+        rows, lanes = by_rows(PR), by_lanes(PR)
+        for name in ("xZY", "xY", "PY"):
+            put(send, table, name, 0, rows)
+        for name in ("xZ", "PZ"):
+            put(send, table, name, 0, lanes)
+        put(send, table, "ZY", 5, rows[0:2])
+        for c in range(2):
+            put(send, table, "x", 8 * c, PR[c])
         return PR
 
     def merge_faces(recv, table, w):
@@ -254,40 +278,36 @@
     at_zym = (lane == 118) & (sub == 7)
     at_yzm = (lane == 6) & (sub == 0)
 
-    def upper(base, vz, vy, vzy):
-        base = jnp.where(at_z, roll(vz, 112), base)
-        base = jnp.where(at_y, roll(vy, 6), base)
-        return jnp.where(at_zy, roll(vzy, 118), base)
+    def upper(base, k, vz, vy, vzy, kzy=None):
+        kzy = k if kzy is None else kzy
+        base = jnp.where(at_z, roll(vz, 112 - 16 * k), base)
+        base = jnp.where(at_y, roll(roll(vy, -k, 0), 6), base)
+        return jnp.where(at_zy, roll(roll(vzy, -kzy, 0), 118), base)
 
     def lower(base, recv, table, c):
-        base = jnp.where(at_zm, roll(get(recv, table, "Xz", c * 8), -112), base)
-        base = jnp.where(at_ym, roll(get(recv, table, "Xy", c * 8), -6), base)
-        base = jnp.where(at_zym, roll(get(recv, table, "XZy", c * 8), 106), base)
-        return jnp.where(at_yzm, roll(get(recv, table, "XzY", c * 8), -106), base)
+        base = jnp.where(at_zm, roll(get(recv, table, "Xz", 0), -112 + 16 * c), base)
+        base = jnp.where(at_ym, roll(roll(get(recv, table, "Xy", 0), c, 0), -6), base)
+        base = jnp.where(at_zym, roll(roll(get(recv, table, "XZy", 0), c, 0), 106), base)
+        return jnp.where(at_yzm, roll(roll(get(recv, table, "XzY", 0), -c, 0), -106), base)
 
     def merge_columns(recv, table, w, PR, ES, EJ):
         first = w == 0
         n = 5 if first else 2
 
-        def ext(at):
-            v = [get(recv, table, name, at) for name in ("X", "XZ", "XY", "XZY")]
-            return upper(*v)
-
-        EK = [ext((n - 2 + c) * 8) for c in range(2)]
+        def ext(k):
+            base = get(recv, table, "X", 8 * k)
+            return upper(base, k, *[get(recv, table, name, 0) for name in ("XZ", "XY", "XZY")])
+
+        EK = [ext(n - 2 + c) for c in range(2)]
         if first:
-            ES = [ext(c * 8) for c in range(2)]
-            EJ = ext(16)
+            ES = [ext(c) for c in range(2)]
+            EJ = ext(2)
         ES = [lower(ES[c], recv, table, c) for c in range(2)]
-        HM = [upper(*[get(recv, table, name, c * 8) for name in ("x", "xZ", "xY", "xZY")]) for c in range(2)]
-        PM = [
-            upper(
-                PR[c],
-                get(recv, table, "Z", n * NY + c * 8),
-                get(recv, table, "Y", n * NZ + c * 8),
-                get(recv, table, "ZY", 8 + c * 8),
-            )
+        HM = [
+            upper(get(recv, table, "x", 8 * c), c, *[get(recv, table, name, 0) for name in ("xZ", "xY", "xZY")])
             for c in range(2)
         ]
+        PM = [upper(PR[c], c, *[get(recv, table, name, 0) for name in ("PZ", "PY", "ZY")], kzy=5 + c) for c in range(2)]
         return EK, ES, EJ, HM, PM
 
     def shift_up(v):
@@ -314,13 +334,11 @@
                 ES = [jnp.where(member, local[c] * scale, ES[c]) for c in range(2)]
         return ES
 
-    def spread_columns(HM, ES):
-        for c in range(2):
-            e = roll(ES[c], -1)
-            even = (lane & 1) == 0
-            mixed = [jnp.where(even, HM[c], e), jnp.where(even, e, HM[c])]
+    def spread(which, values):
+        for c in range(2):
+            v = values[c] if which == 0 else roll(values[c], -1)
             for q in range(TILES, 18 * TILES):
-                XH[c, pl.ds(8 * q, 8), :] = roll(mixed[q % 2], -q)
+                XH[2 * which + c, pl.ds(8 * q, 8), :] = roll(v, -q)
 
     def update(w, base, n, stride, xp):
         def at(off):
@@ -332,7 +350,7 @@
         local, centre = [], []
         for c in range(2):
             v = S[c, at(0), :]
-            edge = XH[c, at(0), :]
+            edge = XH[2 * xp + c, at(0), :]
             left, right = roll(v, 1), roll(v, -1)
             if xp == 0:
                 left = jnp.where(lanes == 0, edge, left)
@@ -370,33 +388,34 @@
         copies_a[name].start()
     each(lambda z: load(z, 3).wait())
     PK = [pack_first(lambda r, c=c: K[2 + c, pl.ds(r, 8), :]) for c in range(2)]
-    for name in NAMES:
+    for name in COLUMNS:
+        copies_a[name].wait_recv()
+    EK, ES, EJ, HM, PM = merge_columns(recv_a, TABLE_A, 0, PR, None, None)
+    spread(0, HM)
+    ES = update_column(EK, ES, EJ, PM)
+    spread(1, ES)
+    for name in FACES:
         copies_a[name].wait_recv()
     merge_faces(recv_a, TABLE_A, 0)
-    EK, ES, EJ, HM, PM = merge_columns(recv_a, TABLE_A, 0, PR, None, None)
-    ES = update_column(EK, ES, EJ, PM)
-    spread_columns(HM, ES)
     for t in range(8):
         section(0, t // 4, t // 2 % 2, t % 2)
 
+    PR = build_columns(send_b, TABLE_B, 1, PJ, PK)
     build(send_b, TABLE_B, 1)
-    PR = build_columns(send_b, TABLE_B, 1, PJ, PK)
     for name in NAMES:
         copies_b[name].start()
     for name in NAMES:
         copies_a[name].wait_send()
-    for name in NAMES:
+    for name in FACES + tuple(COLUMNS):
         copies_b[name].wait_recv()
     merge_faces(recv_b, TABLE_B, 1)
     EK, ES, EJ, HM, PM = merge_columns(recv_b, TABLE_B, 1, PR, ES, EJ)
+    spread(0, HM)
+    section(1, 0, 0, 0)
     ES = update_column(EK, ES, EJ, PM)
-    spread_columns(HM, ES)
-    for t in range(8):
+    spread(1, ES)
+    for t in range(1, 8):
         section(1, t // 4, t // 2 % 2, t % 2)
-
-    def store(z):
-        src = pl.ds(pl.multiple_of((z + 1) * PITCH, 8), NY)
-        return pltpu.make_async_copy(S.at[:, src, :], out.at[:, z], out_sem.at[z])
 
     sums = jnp.sum(jnp.sum(EN[...], axis=1), axis=1, keepdims=True)
     diagonal = lax.broadcasted_iota(jnp.int32, (16, 128), 0) == lax.broadcasted_iota(jnp.int32, (16, 128), 1)
@@ -405,20 +424,22 @@
     erow[0] = mine
     ebuf[index] = mine
 
-    def share(i, carry):
-        to = lax.rem(index + i, total)
+    coords = [[lax.rem(m + d, n) for d in range(n)] for m, n in zip(me, dims)]
+    far = [[min(d, n - d) for d in range(n)] for n in dims]
+    targets = [(a, b, c) for a in range(nz) for b in range(ny) for c in range(nx) if a + b + c]
+    targets.sort(key=lambda t: -(far[0][t[0]] + far[1][t[1]] + (far[2][t[2]] + 1) // 2))
+    for a, b, c in targets:
         pltpu.make_async_remote_copy(
             src_ref=erow.at[0],
             dst_ref=ebuf.at[index],
             send_sem=es_sem,
             recv_sem=er_sem,
-            device_id=(to // (ny * nx), lax.rem(to // nx, ny), lax.rem(to, nx)),
+            device_id=(coords[0][a], coords[1][b], coords[2][c]),
             device_id_type=MESH,
         ).start()
-        return carry
-
-    lax.fori_loop(1, total, share, 0)
-    each(lambda z: store(z).start())
+    for z in range(NZ):
+        for c in range(2):
+            out[c, z] = S[c, pl.ds(row(z, 0), NY), :]
     for name in NAMES:
         copies_b[name].wait_send()
     rest = pl.ds(0, total - 1)
@@ -431,13 +452,15 @@
         device_id_type=MESH,
     )
     done.wait_recv()
-    whole = ebuf[0]
-    for i in range(1, total):
-        whole = whole + ebuf[i]
-    sites = float(8 // 8 * (NZ * nz) * (NY * ny) * (NX * nx) // 8)
-    energy_out[...] = -whole / sites
+    parts = [ebuf[i] for i in range(8)]
+    for i in range(8, total):
+        parts[i % 8] = parts[i % 8] + ebuf[i]
+    while len(parts) > 1:
+        parts = [a + b for a, b in zip(parts[::2], parts[1::2])]
+    whole = parts[0]
+    sites = float((NZ * nz) * (NY * ny) * (NX * nx) // 8)
+    energy_out[...] = (-whole / sites)[0, :16]
     done.wait_send()
-    each(lambda z: store(z).wait())
 
 
 def body(dims, spins, kicks, stiffness):
@@ -448,15 +471,15 @@
         functools.partial(kernel, dims),
         out_shape=(
             jax.ShapeDtypeStruct((2, NZ, NY, NX), F32),
-            jax.ShapeDtypeStruct((1, 128), F32),
+            jax.ShapeDtypeStruct((16,), F32),
         ),
         in_specs=[hbm] * 3,
-        out_specs=(hbm, pl.BlockSpec(memory_space=vmem)),
+        out_specs=(pl.BlockSpec(memory_space=vmem), pl.BlockSpec(memory_space=vmem)),
         scratch_shapes=[
             vmem((2, ROWS, 128), F32),
             vmem((ROWS, 128), F32),
             vmem((4, ROWS, 128), F32),
-            vmem((2, ROWS, 128), F32),
+            vmem((4, ROWS, 128), F32),
             vmem((SIZE_A, 128), F32),
             vmem((SIZE_A, 128), F32),
             vmem((SIZE_B, 128), F32),
@@ -465,7 +488,6 @@
             vmem((total, 1, 128), F32),
             vmem((1, 1, 128), F32),
             dma((4, NZ)),
-            dma((NZ,)),
             dma((COUNT,)),
             dma((COUNT,)),
             dma((COUNT,)),
@@ -473,9 +495,9 @@
             dma,
             dma,
         ],
-        compiler_params=pltpu.CompilerParams(collective_id=0, has_side_effects=True),
-    )(spins, kicks, stiffness)
-    return final, energy[0, :16]
+        compiler_params=pltpu.CompilerParams(collective_id=0, has_side_effects=True, vmem_limit_bytes=12 * 1024 * 1024),
+    )(*[pltpu.with_memory_space_constraint(v, pltpu.HBM) for v in (spins, kicks, stiffness)])
+    return final, energy
 
 
 def solution(mesh):

time: 39.6 us -> 32 us (0.81)
  Pallas kernels: 35.5 us -> 29.8 us
  local copies, waits for them, and re-layouts: 3.15 us -> 1.39 us
    pallas_call x1, Pallas kernels: 35.5 us -> 29.8 us  [body(): pl.pallas_call(functools.partial(kernel, dims), out_shape=(jax.ShapeDtype...]
    squeeze x1 -> x0, local copies, waits for them, and re-layouts: 1.09 us -> none  [body(): return (final, energy[0, :16])]
    unnamed x1 -> x2, local copies, waits for them, and re-layouts: 2.06 us -> 1.39 us
where the time goes in v1:
time: 32 us; the launch traced here: 31.8 us
  Pallas kernels  29.8 us (93%)
  local copies, waits for them, and re-layouts  1.39 us (4%)
  between operations  0.64 us (2%)
    pallas_call x1, Pallas kernels, body(): pl.pallas_call(functools.partial(kernel, dims), out_shape=(jax.ShapeDtype...  29.8 us
    unnamed x2, local copies, waits for them, and re-layouts  1.39 us

profile of v1, /device:TPU:1, one launch (start us, length us, event | category | flops | bytes accessed | tf_op | source)
XLA Modules:
  0.0 31.8 jit_solution(7612624487484566897)
XLA Ops:
  0.6 29.8 %shard_map.50 = (f32[2,16,48,128]{3,2,1,0:T(8,128)S(1)}, f32[16]{0:T(128)S(1)}) custom-call(f32[2,16,48,128]{3,2,1,0:T(8,128)} %spins.1, f32[2,2,16,48,128]{4,3,2,1,0:T(8,128)} %kicks.1, f32[16,48,128]{2,1,0:T(8,128)} %stiff.1), custom_call_target="tpu_custom_call" | custom-call | tf_op jit(solution)/shard_map/pallas_call | solution.py:470
  30.4 0.9 %copy.7 = f32[2,16,48,128]{3,2,1,0:T(8,128)} copy(f32[2,16,48,128]{3,2,1,0:T(8,128)S(1)} %get-tuple-element.4) | data formatting | bytes 1572864
  31.3 0.5 %copy.8 = f32[16]{0:T(128)} copy(f32[16]{0:T(128)S(1)} %get-tuple-element.5) | data formatting | bytes 128

commit v2 on v1

--- a/solution.py
+++ b/solution.py
@@ -65,7 +65,7 @@
     return v if shift == 0 else pltpu.roll(v, shift, axis)
 
 
-def kernel(dims, spins, kicks, stiff, out, energy_out, S, J, K, XH, send_a, recv_a, send_b, recv_b, EN, ebuf, erow,
+def kernel(dims, spins, kicks, stiff, out, energy_out, S, J, K, XH, fold, send_a, recv_a, send_b, recv_b, EN, ebuf, erow,
            load_sem, sa_sem, ra_sem, sb_sem, rb_sem, es_sem, er_sem):
     nz, ny, nx = dims
     total = nz * ny * nx
@@ -79,24 +79,17 @@
     zi = (lane * 9363) >> 16
     tile = lane - zi * 7
 
-    def load(z, which):
-        dst = pl.ds(pl.multiple_of((z + 1) * PITCH, 8), NY)
-        if which == 0:
-            return pltpu.make_async_copy(spins.at[:, z], S.at[:, dst, :], load_sem.at[0, z])
-        if which == 1:
-            return pltpu.make_async_copy(stiff.at[z], J.at[dst, :], load_sem.at[1, z])
-        w = which - 2
-        return pltpu.make_async_copy(kicks.at[w, :, z], K.at[pl.ds(2 * w, 2), dst, :], load_sem.at[which, z])
-
-    def each(f):
-        def step(z, carry):
-            f(z)
-            return carry
-
-        lax.fori_loop(0, NZ, step, 0)
-
-    for which in range(4):
-        each(lambda z, which=which: load(z, which).start())
+    inner = (pl.ds(1, NZ), pl.ds(0, NY))
+    planes = ROWS // PITCH
+    loads = [
+        pltpu.make_async_copy(spins, S.reshape(2, planes, PITCH, 128).at[(slice(None),) + inner], load_sem.at[0]),
+        pltpu.make_async_copy(stiff, J.reshape(planes, PITCH, 128).at[inner], load_sem.at[1]),
+    ]
+    for w in range(2):
+        whole = K.reshape(4, planes, PITCH, 128)
+        loads.append(pltpu.make_async_copy(kicks.at[w], whole.at[(pl.ds(2 * w, 2),) + inner], load_sem.at[2 + w]))
+    for copy in loads:
+        copy.start()
 
     barrier = pltpu.get_barrier_semaphore()
     steps = sorted({MESSAGES[name][0] for name in NAMES})
@@ -104,8 +97,8 @@
     for s in steps:
         pl.semaphore_signal(barrier, inc=1, device_id=device(tuple(-d for d in s)), device_id_type=MESH)
 
-    for which in range(3):
-        each(lambda z, which=which: load(z, which).wait())
+    for copy in loads[:3]:
+        copy.wait()
 
     zero_plane = jnp.zeros((PITCH, 128), F32)
     for c in range(2):
@@ -335,12 +328,17 @@
         return ES
 
     def spread(which, values):
-        for c in range(2):
-            v = values[c] if which == 0 else roll(values[c], -1)
-            for q in range(TILES, 18 * TILES):
-                XH[2 * which + c, pl.ds(8 * q, 8), :] = roll(v, -q)
-
-    def update(w, base, n, stride, xp):
+        result = []
+        for c in range(2):
+            v = values[c]
+            fold[2 * which + c, 0:8] = v
+            fold[2 * which + c, 8:16] = roll(v, -1)
+            result.append([fold[2 * which + c, pl.ds(yp, 8, stride=2)] for yp in range(2)])
+            for z in range(NZ + 1):
+                XH[2 * which + c, pl.ds(z, 1), :] = roll(v, 127 * which - ((z + 1) * TILES + 6))[0:1]
+        return result
+
+    def update(w, base, n, stride, xp, edges):
         def at(off):
             return pl.ds(base + off, n, stride=stride) if n > 1 else pl.ds(base + off, 1)
 
@@ -350,7 +348,7 @@
         local, centre = [], []
         for c in range(2):
             v = S[c, at(0), :]
-            edge = XH[2 * xp + c, at(0), :]
+            edge = edges[c]
             left, right = roll(v, 1), roll(v, -1)
             if xp == 0:
                 left = jnp.where(lanes == 0, edge, left)
@@ -365,16 +363,21 @@
             S[c, at(0), :] = jnp.where(member, local[c] * scale, centre[c])
         return q * scale
 
-    def section(w, zp, yp, xp):
+    def section(w, zp, yp, xp, columns):
         energy = None
         for z in range(zp, NZ + 1 - zp, 2):
-            e = update(w, row(z, yp), 24, 2, xp)
+            first = 127 * xp - (z + 1) * TILES
+            edges = [
+                jnp.concatenate([roll(columns[c][yp], first - 2 * j) for j in range(3)], axis=0) for c in range(2)
+            ]
+            e = update(w, row(z, yp), 24, 2, xp, edges)
             if z < NZ:
                 energy = e if energy is None else energy + e
         if yp == 0:
-            update(w, row(zp, 48), 8, 2 * PITCH, xp)
+            edges = [XH[2 * xp + c, pl.ds(zp, 8, stride=2), :] for c in range(2)]
+            update(w, row(zp, 48), 8, 2 * PITCH, xp, edges)
             if zp == 0:
-                update(w, row(16, 48), 1, 1, xp)
+                update(w, row(16, 48), 1, 1, xp, [XH[2 * xp + c, pl.ds(NZ, 1), :] for c in range(2)])
         energy = energy[0:8] + energy[8:16] + energy[16:24]
         t = 8 * w + 4 * zp + 2 * yp + xp
         EN[t] = jnp.where((lane & 1) == xp, energy, 0.0)
@@ -386,19 +389,19 @@
     pl.semaphore_wait(barrier, len(steps))
     for name in NAMES:
         copies_a[name].start()
-    each(lambda z: load(z, 3).wait())
+    loads[3].wait()
     PK = [pack_first(lambda r, c=c: K[2 + c, pl.ds(r, 8), :]) for c in range(2)]
     for name in COLUMNS:
         copies_a[name].wait_recv()
     EK, ES, EJ, HM, PM = merge_columns(recv_a, TABLE_A, 0, PR, None, None)
-    spread(0, HM)
+    columns = [spread(0, HM)]
     ES = update_column(EK, ES, EJ, PM)
-    spread(1, ES)
+    columns.append(spread(1, ES))
     for name in FACES:
         copies_a[name].wait_recv()
     merge_faces(recv_a, TABLE_A, 0)
     for t in range(8):
-        section(0, t // 4, t // 2 % 2, t % 2)
+        section(0, t // 4, t // 2 % 2, t % 2, columns[t % 2])
 
     PR = build_columns(send_b, TABLE_B, 1, PJ, PK)
     build(send_b, TABLE_B, 1)
@@ -410,12 +413,12 @@
         copies_b[name].wait_recv()
     merge_faces(recv_b, TABLE_B, 1)
     EK, ES, EJ, HM, PM = merge_columns(recv_b, TABLE_B, 1, PR, ES, EJ)
-    spread(0, HM)
-    section(1, 0, 0, 0)
+    columns = [spread(0, HM)]
+    section(1, 0, 0, 0, columns[0])
     ES = update_column(EK, ES, EJ, PM)
-    spread(1, ES)
+    columns.append(spread(1, ES))
     for t in range(1, 8):
-        section(1, t // 4, t // 2 % 2, t % 2)
+        section(1, t // 4, t // 2 % 2, t % 2, columns[t % 2])
 
     sums = jnp.sum(jnp.sum(EN[...], axis=1), axis=1, keepdims=True)
     diagonal = lax.broadcasted_iota(jnp.int32, (16, 128), 0) == lax.broadcasted_iota(jnp.int32, (16, 128), 1)
@@ -479,7 +482,8 @@
             vmem((2, ROWS, 128), F32),
             vmem((ROWS, 128), F32),
             vmem((4, ROWS, 128), F32),
-            vmem((4, ROWS, 128), F32),
+            vmem((4, 24, 128), F32),
+            vmem((4, 16, 128), F32),
             vmem((SIZE_A, 128), F32),
             vmem((SIZE_A, 128), F32),
             vmem((SIZE_B, 128), F32),
@@ -487,7 +491,7 @@
             vmem((16, 8, 128), F32),
             vmem((total, 1, 128), F32),
             vmem((1, 1, 128), F32),
-            dma((4, NZ)),
+            dma((4,)),
             dma((COUNT,)),
             dma((COUNT,)),
             dma((COUNT,)),
@@ -497,7 +501,22 @@
         ],
         compiler_params=pltpu.CompilerParams(collective_id=0, has_side_effects=True, vmem_limit_bytes=12 * 1024 * 1024),
     )(*[pltpu.with_memory_space_constraint(v, pltpu.HBM) for v in (spins, kicks, stiffness)])
-    return final, energy
+    def finish(final, energy, out, energy_out, sem):
+        copies = [pltpu.make_async_copy(final, out, sem.at[0]), pltpu.make_async_copy(energy, energy_out, sem.at[1])]
+        for copy in copies:
+            copy.start()
+        for copy in copies:
+            copy.wait()
+
+    final, energy = [pltpu.with_memory_space_constraint(v, pltpu.VMEM) for v in (final, energy)]
+    return pl.pallas_call(
+        finish,
+        out_shape=(jax.ShapeDtypeStruct((2, NZ, NY, NX), F32), jax.ShapeDtypeStruct((16,), F32)),
+        in_specs=[hbm, hbm],
+        out_specs=(hbm, hbm),
+        scratch_shapes=[dma((2,))],
+        compiler_params=pltpu.CompilerParams(vmem_limit_bytes=1024 * 1024),
+    )(final, energy)
 
 
 def solution(mesh):

time: 32 us -> 30.9 us (0.966)
  local copies, waits for them, and re-layouts: 1.39 us -> 0 us
    unnamed x2 -> x0, local copies, waits for them, and re-layouts: 1.39 us -> none
    pallas_call x0 -> x1, Pallas kernels: none -> 0.9 us  [body(): pl.pallas_call(finish, out_shape=(jax.ShapeDtypeStruct((2, NZ, NY, NX), F...]
    pallas_call x1, Pallas kernels: 29.8 us -> 29.2 us  [body(): pl.pallas_call(functools.partial(kernel, dims), out_shape=(jax.ShapeDtype...]
where the time goes in v2:
time: 30.9 us; the launch traced here: 30.8 us
  Pallas kernels  30.1 us (97%)
  between operations  0.64 us (2%)
    pallas_call x1, Pallas kernels, body(): pl.pallas_call(functools.partial(kernel, dims), out_shape=(jax.ShapeDtype...  29.2 us
    pallas_call x1, Pallas kernels, body(): pl.pallas_call(finish, out_shape=(jax.ShapeDtypeStruct((2, NZ, NY, NX), F...  0.9 us

profile of v2, /device:TPU:1, one launch (start us, length us, event | category | flops | bytes accessed | tf_op | source)
XLA Modules:
  0.0 30.8 jit_solution(18221361781075884868)
XLA Ops:
  0.6 29.2 %shard_map.50 = (f32[2,16,48,128]{3,2,1,0:T(8,128)S(1)}, f32[16]{0:T(128)S(1)}) custom-call(f32[2,16,48,128]{3,2,1,0:T(8,128)} %spins.1, f32[2,2,16,48,128]{4,3,2,1,0:T(8,128)} %kicks.1, f32[16,48,128]{2,1,0:T(8,128)} %stiff.1), custom_call_target="tpu_custom_call" | custom-call | tf_op jit(solution)/shard_map/pallas_call | solution.py:473
  29.9 0.9 %shard_map.51 = (f32[2,16,48,128]{3,2,1,0:T(8,128)}, f32[16]{0:T(128)}) custom-call(f32[2,16,48,128]{3,2,1,0:T(8,128)S(1)} %get-tuple-element.4.final, f32[16]{0:T(128)S(1)} %get-tuple-element.5.energy), custom_call_target="tpu_custom_call" | custom-call | tf_op jit(solution)/shard_map/pallas_call | solution.py:512

commit v3 on v2

--- a/solution.py
+++ b/solution.py
@@ -32,15 +32,23 @@
     "PY": ((0, -1, 0), 8, 8),
     "X": ((0, 0, -1), 40, 16),
     "x": ((0, 0, 1), 16, 16),
-    "Z": ((-1, 0, 0), 240, 96),
     "z": ((1, 0, 0), 96, 96),
     "Y": ((0, -1, 0), 80, 32),
     "y": ((0, 1, 0), 32, 32),
+    "Z": ((-1, 0, 0), 96, 96),
+    "ZS": ((-1, 0, 0), 144, 0),
 }
 NAMES = list(MESSAGES)
 COUNT = len(NAMES)
-FACES = ("Zy", "zY", "Z", "z", "Y", "y")
-COLUMNS = [name for name in NAMES if name not in FACES]
+TOP = ("Z", "ZS")
+FACES = ("Zy", "zY", "z", "Y", "y")
+LEFT = ("x", "xZ", "xY", "ZY")
+RIGHT = [name for name in NAMES if name not in FACES + TOP + LEFT + ("xZY",)]
+NAMES_B = [name for name in NAMES if name != "ZS"]
+
+
+def away(name):
+    return sum(abs(d) for d in MESSAGES[name][0])
 
 
 def offsets(round_index):
@@ -66,7 +74,7 @@
 
 
 def kernel(dims, spins, kicks, stiff, out, energy_out, S, J, K, XH, fold, send_a, recv_a, send_b, recv_b, EN, ebuf, erow,
-           load_sem, sa_sem, ra_sem, sb_sem, rb_sem, es_sem, er_sem):
+           load_sem, token, sa_sem, ra_sem, sb_sem, rb_sem, es_sem, er_sem):
     nz, ny, nx = dims
     total = nz * ny * nx
     me = (lax.axis_index("gz"), lax.axis_index("gy"), lax.axis_index("gx"))
@@ -92,8 +100,9 @@
         copy.start()
 
     barrier = pltpu.get_barrier_semaphore()
-    steps = sorted({MESSAGES[name][0] for name in NAMES})
+    steps = sorted({MESSAGES[name][0] for name in NAMES if away(name) < 3})
     steps += [(0, 0, d) for d in range(2, nx - 1)]
+    steps.sort(key=lambda step: -sum(map(abs, step)))
     for s in steps:
         pl.semaphore_signal(barrier, inc=1, device_id=device(tuple(-d for d in s)), device_id_type=MESH)
 
@@ -142,6 +151,8 @@
         result = {}
         for i, name in enumerate(NAMES):
             start, size = table[name]
+            if size == 0:
+                continue
             part = pl.ds(start, size)
             result[name] = pltpu.make_async_remote_copy(
                 src_ref=send.at[part, :],
@@ -168,12 +179,12 @@
         J0 = J[pl.ds(row(0, 0), NY), :]
         for c in range(2):
             kc = K[2 * w + c, pl.ds(row(0, 0), NY), :] + J0 * S[c, pl.ds(row(1, 0), NY), :]
-            put(send, table, "Z", (n - 2 + c) * NY, kc)
+            put(send, table, "Z", c * NY, kc)
             if first:
-                put(send, table, "Z", c * NY, S[c, pl.ds(row(0, 0), NY), :])
+                put(send, table, "ZS", c * NY, S[c, pl.ds(row(0, 0), NY), :])
             put(send, table, "z", c * NY, S[c, pl.ds(row(15, 0), NY), :])
         if first:
-            put(send, table, "Z", 2 * NY, J0)
+            put(send, table, "ZS", 2 * NY, J0)
         rows0 = pl.ds(row(0, 0), NZ, stride=PITCH)
         rows1 = pl.ds(row(0, 1), NZ, stride=PITCH)
         rows47 = pl.ds(row(0, 47), NZ, stride=PITCH)
@@ -243,15 +254,12 @@
     def merge_faces(recv, table, w):
         first = w == 0
         n = 5 if first else 2
-        plane = pl.ds(row(16, 0), NY)
         rows48 = pl.ds(row(0, 48), NZ, stride=PITCH)
         at = pl.ds(row(16, 48), 1)
         for c in range(2):
-            K[2 * w + c, plane, :] = get(recv, table, "Z", (n - 2 + c) * NY, NY)
             K[2 * w + c, rows48, :] = get(recv, table, "Y", (n - 2 + c) * NZ, NZ)
             K[2 * w + c, at, :] = get(recv, table, "ZY", n - 2 + c, 1)
             if first:
-                S[c, plane, :] = get(recv, table, "Z", c * NY, NY)
                 S[c, rows48, :] = get(recv, table, "Y", c * NZ, NZ)
                 S[c, at, :] = get(recv, table, "ZY", c, 1)
             S[c, pl.ds(row(-1, 0), NY), :] = get(recv, table, "z", c * NY, NY)
@@ -259,9 +267,17 @@
             S[c, pl.ds(row(16, -1), 1), :] = get(recv, table, "Zy", c, 1)
             S[c, pl.ds(row(-1, 48), 1), :] = get(recv, table, "zY", c, 1)
         if first:
-            J[plane, :] = get(recv, table, "Z", 2 * NY, NY)
             J[rows48, :] = get(recv, table, "Y", 2 * NZ, NZ)
             J[at, :] = get(recv, table, "ZY", 2, 1)
+
+    def merge_top(recv, table, w):
+        plane = pl.ds(row(16, 0), NY)
+        for c in range(2):
+            K[2 * w + c, plane, :] = get(recv, table, "Z", c * NY, NY)
+            if w == 0:
+                S[c, plane, :] = get(recv, table, "ZS", c * NY, NY)
+        if w == 0:
+            J[plane, :] = get(recv, table, "ZS", 2 * NY, NY)
 
     at_z = (zi == 17) & (tile < 6)
     at_y = (tile == 6) & (sub == 0) & (zi >= 1) & (zi <= 16)
@@ -283,6 +299,14 @@
         base = jnp.where(at_zym, roll(roll(get(recv, table, "XZy", 0), c, 0), 106), base)
         return jnp.where(at_yzm, roll(roll(get(recv, table, "XzY", 0), -c, 0), -106), base)
 
+    def merge_left(recv, table):
+        result = []
+        for c in range(2):
+            base = get(recv, table, "x", 8 * c)
+            base = jnp.where(at_z, roll(get(recv, table, "xZ", 0), 112 - 16 * c), base)
+            result.append(jnp.where(at_y, roll(roll(get(recv, table, "xY", 0), -c, 0), 6), base))
+        return result
+
     def merge_columns(recv, table, w, PR, ES, EJ):
         first = w == 0
         n = 5 if first else 2
@@ -296,12 +320,8 @@
             ES = [ext(c) for c in range(2)]
             EJ = ext(2)
         ES = [lower(ES[c], recv, table, c) for c in range(2)]
-        HM = [
-            upper(get(recv, table, "x", 8 * c), c, *[get(recv, table, name, 0) for name in ("xZ", "xY", "xZY")])
-            for c in range(2)
-        ]
         PM = [upper(PR[c], c, *[get(recv, table, name, 0) for name in ("PZ", "PY", "ZY")], kzy=5 + c) for c in range(2)]
-        return EK, ES, EJ, HM, PM
+        return EK, ES, EJ, PM
 
     def shift_up(v):
         v = roll(v, 1, 0)
@@ -334,7 +354,7 @@
             fold[2 * which + c, 0:8] = v
             fold[2 * which + c, 8:16] = roll(v, -1)
             result.append([fold[2 * which + c, pl.ds(yp, 8, stride=2)] for yp in range(2)])
-            for z in range(NZ + 1):
+            for z in range(NZ + which):
                 XH[2 * which + c, pl.ds(z, 1), :] = roll(v, 127 * which - ((z + 1) * TILES + 6))[0:1]
         return result
 
@@ -363,62 +383,80 @@
             S[c, at(0), :] = jnp.where(member, local[c] * scale, centre[c])
         return q * scale
 
+    def edges_of(z, yp, xp, columns):
+        first = 127 * xp - (z + 1) * TILES
+        return [jnp.concatenate([roll(columns[c][yp], first - 2 * j) for j in range(3)], axis=0) for c in range(2)]
+
+    def top(w, yp, xp, columns):
+        update(w, row(NZ, yp), 24, 2, xp, edges_of(NZ, yp, xp, columns))
+        if yp == 0:
+            update(w, row(NZ, 48), 1, 1, xp, [XH[2 * xp + c, pl.ds(NZ, 1), :] for c in range(2)])
+
     def section(w, zp, yp, xp, columns):
         energy = None
-        for z in range(zp, NZ + 1 - zp, 2):
-            first = 127 * xp - (z + 1) * TILES
-            edges = [
-                jnp.concatenate([roll(columns[c][yp], first - 2 * j) for j in range(3)], axis=0) for c in range(2)
-            ]
-            e = update(w, row(z, yp), 24, 2, xp, edges)
-            if z < NZ:
-                energy = e if energy is None else energy + e
+        for z in range(zp, NZ, 2):
+            e = update(w, row(z, yp), 24, 2, xp, edges_of(z, yp, xp, columns))
+            energy = e if energy is None else energy + e
         if yp == 0:
             edges = [XH[2 * xp + c, pl.ds(zp, 8, stride=2), :] for c in range(2)]
             update(w, row(zp, 48), 8, 2 * PITCH, xp, edges)
-            if zp == 0:
-                update(w, row(16, 48), 1, 1, xp, [XH[2 * xp + c, pl.ds(NZ, 1), :] for c in range(2)])
         energy = energy[0:8] + energy[8:16] + energy[16:24]
         t = 8 * w + 4 * zp + 2 * yp + xp
         EN[t] = jnp.where((lane & 1) == xp, energy, 0.0)
+
+    def sweep(w, copies, recv, table, PR, ES, EJ):
+        def arrived(names):
+            for name in names:
+                if name in copies:
+                    copies[name].wait_recv()
+
+        arrived(LEFT + FACES)
+        merge_faces(recv, table, w)
+        left = spread(0, merge_left(recv, table))
+        section(w, 0, 0, 0, left)
+        section(w, 0, 1, 0, left)
+        arrived(("xZY",) + TOP)
+        merge_top(recv, table, w)
+        corner = roll(get(recv, table, "xZY", 0), -TILES)
+        for c in range(2):
+            XH[c, pl.ds(NZ, 1), :] = corner[c : c + 1]
+        for yp in range(2):
+            top(w, yp, 0, left)
+            section(w, 1, yp, 0, left)
+        arrived(RIGHT)
+        EK, ES, EJ, PM = merge_columns(recv, table, w, PR, ES, EJ)
+        ES = update_column(EK, ES, EJ, PM)
+        right = spread(1, ES)
+        for zp in range(2):
+            for yp in range(2):
+                if zp == 1:
+                    top(w, yp, 1, right)
+                section(w, zp, yp, 1, right)
+        return ES, EJ
 
     build(send_a, TABLE_A, 0)
     PJ = pack_first(lambda r: J[pl.ds(r, 8), :])
     PK = [pack_first(lambda r, c=c: K[c, pl.ds(r, 8), :]) for c in range(2)]
     PR = build_columns(send_a, TABLE_A, 0, PJ, PK)
     pl.semaphore_wait(barrier, len(steps))
-    for name in NAMES:
+    for step in ((0, 0, -1), (0, 0, 1)):
+        pl.semaphore_signal(token, inc=1, device_id=device(step), device_id_type=MESH)
+    for name in [name for name in NAMES if away(name) < 3 and name not in TOP]:
+        copies_a[name].start()
+    pl.semaphore_wait(token, 2)
+    for name in [name for name in NAMES if away(name) == 3] + ["Z", "ZS"]:
         copies_a[name].start()
     loads[3].wait()
     PK = [pack_first(lambda r, c=c: K[2 + c, pl.ds(r, 8), :]) for c in range(2)]
-    for name in COLUMNS:
-        copies_a[name].wait_recv()
-    EK, ES, EJ, HM, PM = merge_columns(recv_a, TABLE_A, 0, PR, None, None)
-    columns = [spread(0, HM)]
-    ES = update_column(EK, ES, EJ, PM)
-    columns.append(spread(1, ES))
-    for name in FACES:
-        copies_a[name].wait_recv()
-    merge_faces(recv_a, TABLE_A, 0)
-    for t in range(8):
-        section(0, t // 4, t // 2 % 2, t % 2, columns[t % 2])
+    ES, EJ = sweep(0, copies_a, recv_a, TABLE_A, PR, None, None)
 
     PR = build_columns(send_b, TABLE_B, 1, PJ, PK)
     build(send_b, TABLE_B, 1)
-    for name in NAMES:
+    for name in NAMES_B:
         copies_b[name].start()
     for name in NAMES:
         copies_a[name].wait_send()
-    for name in FACES + tuple(COLUMNS):
-        copies_b[name].wait_recv()
-    merge_faces(recv_b, TABLE_B, 1)
-    EK, ES, EJ, HM, PM = merge_columns(recv_b, TABLE_B, 1, PR, ES, EJ)
-    columns = [spread(0, HM)]
-    section(1, 0, 0, 0, columns[0])
-    ES = update_column(EK, ES, EJ, PM)
-    columns.append(spread(1, ES))
-    for t in range(1, 8):
-        section(1, t // 4, t // 2 % 2, t % 2, columns[t % 2])
+    sweep(1, copies_b, recv_b, TABLE_B, PR, ES, EJ)
 
     sums = jnp.sum(jnp.sum(EN[...], axis=1), axis=1, keepdims=True)
     diagonal = lax.broadcasted_iota(jnp.int32, (16, 128), 0) == lax.broadcasted_iota(jnp.int32, (16, 128), 1)
@@ -443,7 +481,7 @@
     for z in range(NZ):
         for c in range(2):
             out[c, z] = S[c, pl.ds(row(z, 0), NY), :]
-    for name in NAMES:
+    for name in NAMES_B:
         copies_b[name].wait_send()
     rest = pl.ds(0, total - 1)
     done = pltpu.make_async_remote_copy(
@@ -492,6 +530,7 @@
             vmem((total, 1, 128), F32),
             vmem((1, 1, 128), F32),
             dma((4,)),
+            pltpu.SemaphoreType.REGULAR,
             dma((COUNT,)),
             dma((COUNT,)),
             dma((COUNT,)),

time: 30.9 us -> 30.8 us (level)
  no operation moved by 1% of the time
where the time goes in v3:
time: 30.8 us; the launch traced here: 30.7 us
  Pallas kernels  30 us (97%)
  between operations  0.64 us (2%)
    pallas_call x1, Pallas kernels, body(): pl.pallas_call(functools.partial(kernel, dims), out_shape=(jax.ShapeDtype...  29.1 us
    pallas_call x1, Pallas kernels, body(): pl.pallas_call(finish, out_shape=(jax.ShapeDtypeStruct((2, NZ, NY, NX), F...  0.9 us

profile of v3, /device:TPU:1, one launch (start us, length us, event | category | flops | bytes accessed | tf_op | source)
XLA Modules:
  0.0 30.7 jit_solution(17468188027227591762)
XLA Ops:
  0.6 29.1 %shard_map.50 = (f32[2,16,48,128]{3,2,1,0:T(8,128)S(1)}, f32[16]{0:T(128)S(1)}) custom-call(f32[2,16,48,128]{3,2,1,0:T(8,128)} %spins.1, f32[2,2,16,48,128]{4,3,2,1,0:T(8,128)} %kicks.1, f32[16,48,128]{2,1,0:T(8,128)} %stiff.1), custom_call_target="tpu_custom_call" | custom-call | tf_op jit(solution)/shard_map/pallas_call | solution.py:511
  29.8 0.9 %shard_map.51 = (f32[2,16,48,128]{3,2,1,0:T(8,128)}, f32[16]{0:T(128)}) custom-call(f32[2,16,48,128]{3,2,1,0:T(8,128)S(1)} %get-tuple-element.4.final, f32[16]{0:T(128)S(1)} %get-tuple-element.5.energy), custom_call_target="tpu_custom_call" | custom-call | tf_op jit(solution)/shard_map/pallas_call | solution.py:551

commit v4 on v3

--- a/solution.py
+++ b/solution.py
@@ -411,6 +411,10 @@
                     copies[name].wait_recv()
 
         arrived(LEFT + FACES)
+        arrived(RIGHT)
+        EK, ES, EJ, PM = merge_columns(recv, table, w, PR, ES, EJ)
+        ES = update_column(EK, ES, EJ, PM)
+        right = spread(1, ES)
         merge_faces(recv, table, w)
         left = spread(0, merge_left(recv, table))
         section(w, 0, 0, 0, left)
@@ -423,10 +427,6 @@
         for yp in range(2):
             top(w, yp, 0, left)
             section(w, 1, yp, 0, left)
-        arrived(RIGHT)
-        EK, ES, EJ, PM = merge_columns(recv, table, w, PR, ES, EJ)
-        ES = update_column(EK, ES, EJ, PM)
-        right = spread(1, ES)
         for zp in range(2):
             for yp in range(2):
                 if zp == 1:

time: 30.8 us -> 30.2 us (0.981)
  Pallas kernels: 30 us -> 29.4 us
    pallas_call x1, Pallas kernels: 29.1 us -> 28.5 us  [body(): pl.pallas_call(functools.partial(kernel, dims), out_shape=(jax.ShapeDtype...]
where the time goes in v4:
time: 30.2 us; the launch traced here: 30.1 us
  Pallas kernels  29.4 us (97%)
  between operations  0.64 us (2%)
    pallas_call x1, Pallas kernels, body(): pl.pallas_call(functools.partial(kernel, dims), out_shape=(jax.ShapeDtype...  28.5 us
    pallas_call x1, Pallas kernels, body(): pl.pallas_call(finish, out_shape=(jax.ShapeDtypeStruct((2, NZ, NY, NX), F...  0.9 us

profile of v4, /device:TPU:1, one launch (start us, length us, event | category | flops | bytes accessed | tf_op | source)
XLA Modules:
  0.0 30.1 jit_solution(2378511069996332030)
XLA Ops:
  0.6 28.5 %shard_map.50 = (f32[2,16,48,128]{3,2,1,0:T(8,128)S(1)}, f32[16]{0:T(128)S(1)}) custom-call(f32[2,16,48,128]{3,2,1,0:T(8,128)} %spins.1, f32[2,2,16,48,128]{4,3,2,1,0:T(8,128)} %kicks.1, f32[16,48,128]{2,1,0:T(8,128)} %stiff.1), custom_call_target="tpu_custom_call" | custom-call | tf_op jit(solution)/shard_map/pallas_call | solution.py:511
  29.2 0.9 %shard_map.51 = (f32[2,16,48,128]{3,2,1,0:T(8,128)}, f32[16]{0:T(128)}) custom-call(f32[2,16,48,128]{3,2,1,0:T(8,128)S(1)} %get-tuple-element.4.final, f32[16]{0:T(128)S(1)} %get-tuple-element.5.energy), custom_call_target="tpu_custom_call" | custom-call | tf_op jit(solution)/shard_map/pallas_call | solution.py:551

commit v5 on v4

--- a/solution.py
+++ b/solution.py
@@ -404,6 +404,12 @@
         t = 8 * w + 4 * zp + 2 * yp + xp
         EN[t] = jnp.where((lane & 1) == xp, energy, 0.0)
 
+    def row_of_sums():
+        sums = jnp.sum(jnp.sum(EN[0:15], axis=1), axis=1, keepdims=True)
+        lanes = lax.broadcasted_iota(jnp.int32, (15, 128), 1)
+        diagonal = lanes == lax.broadcasted_iota(jnp.int32, (15, 128), 0)
+        return jnp.sum(jnp.where(diagonal, jnp.broadcast_to(sums, (15, 128)), 0.0), axis=0, keepdims=True)
+
     def sweep(w, copies, recv, table, PR, ES, EJ):
         def arrived(names):
             for name in names:
@@ -431,8 +437,9 @@
             for yp in range(2):
                 if zp == 1:
                     top(w, yp, 1, right)
+                early = row_of_sums() if (w, zp, yp) == (1, 1, 1) else None
                 section(w, zp, yp, 1, right)
-        return ES, EJ
+        return ES, EJ, early
 
     build(send_a, TABLE_A, 0)
     PJ = pack_first(lambda r: J[pl.ds(r, 8), :])
@@ -448,7 +455,7 @@
         copies_a[name].start()
     loads[3].wait()
     PK = [pack_first(lambda r, c=c: K[2 + c, pl.ds(r, 8), :]) for c in range(2)]
-    ES, EJ = sweep(0, copies_a, recv_a, TABLE_A, PR, None, None)
+    ES, EJ, _ = sweep(0, copies_a, recv_a, TABLE_A, PR, None, None)
 
     PR = build_columns(send_b, TABLE_B, 1, PJ, PK)
     build(send_b, TABLE_B, 1)
@@ -456,11 +463,10 @@
         copies_b[name].start()
     for name in NAMES:
         copies_a[name].wait_send()
-    sweep(1, copies_b, recv_b, TABLE_B, PR, ES, EJ)
-
-    sums = jnp.sum(jnp.sum(EN[...], axis=1), axis=1, keepdims=True)
-    diagonal = lax.broadcasted_iota(jnp.int32, (16, 128), 0) == lax.broadcasted_iota(jnp.int32, (16, 128), 1)
-    mine = jnp.sum(jnp.where(diagonal, jnp.broadcast_to(sums, (16, 128)), 0.0), axis=0, keepdims=True)
+    _, _, early = sweep(1, copies_b, recv_b, TABLE_B, PR, ES, EJ)
+
+    last = jnp.sum(jnp.sum(EN[15], axis=0, keepdims=True), axis=1, keepdims=True)
+    mine = jnp.where(lane[0:1] == 15, jnp.broadcast_to(last, (1, 128)), early)
     index = (me[0] * ny + me[1]) * nx + me[2]
     erow[0] = mine
     ebuf[index] = mine

time: 30.2 us -> 30.2 us (level)
  no operation moved by 1% of the time
where the time goes in v5:
time: 30.2 us; the launch traced here: 30 us
  Pallas kernels  29.4 us (97%)
  between operations  0.64 us (2%)
    pallas_call x1, Pallas kernels, body(): pl.pallas_call(functools.partial(kernel, dims), out_shape=(jax.ShapeDtype...  28.5 us
    pallas_call x1, Pallas kernels, body(): pl.pallas_call(finish, out_shape=(jax.ShapeDtypeStruct((2, NZ, NY, NX), F...  0.9 us

profile of v5, /device:TPU:1, one launch (start us, length us, event | category | flops | bytes accessed | tf_op | source)
XLA Modules:
  0.0 30.0 jit_solution(17523134913951197873)
XLA Ops:
  0.6 28.5 %shard_map.50 = (f32[2,16,48,128]{3,2,1,0:T(8,128)S(1)}, f32[16]{0:T(128)S(1)}) custom-call(f32[2,16,48,128]{3,2,1,0:T(8,128)} %spins.1, f32[2,2,16,48,128]{4,3,2,1,0:T(8,128)} %kicks.1, f32[16,48,128]{2,1,0:T(8,128)} %stiff.1), custom_call_target="tpu_custom_call" | custom-call | tf_op jit(solution)/shard_map/pallas_call | solution.py:517
  29.1 0.9 %shard_map.51 = (f32[2,16,48,128]{3,2,1,0:T(8,128)}, f32[16]{0:T(128)}) custom-call(f32[2,16,48,128]{3,2,1,0:T(8,128)S(1)} %get-tuple-element.4.final, f32[16]{0:T(128)S(1)} %get-tuple-element.5.energy), custom_call_target="tpu_custom_call" | custom-call | tf_op jit(solution)/shard_map/pallas_call | solution.py:557
